TPU v7x, 256 devices: a whole 4x4x8 slice. The times are simulated.
256 devices in a mesh: grp: 8 (over y, z_hi), dev: 32 (over x, z_lo, core).
Axes of the slice: x: 4, y: 4, z: 8 (z_hi: 2, z_lo: 4; z = z_hi * 4 + z_lo), core: 2. Of those that a mesh axis runs over, the one named last changes fastest.
Arguments:
- sources: bfloat16 [524288, 768], P(('grp', 'dev')), may hold values from -6 to 6
- encoder: bfloat16 [524288, 256], P(('grp', 'dev')), may hold values from -0.125 to 0.125
- section_weight: bfloat16 [256, 5, 2, 256, 256], P(('grp', 'dev')), may hold values from -0.25 to 0.25
- cross_weight: bfloat16 [8, 32, 8, 256, 256], P('grp', 'dev'), may hold values from -0.125 to 0.125
- local_weight: bfloat16 [256, 14, 256, 256], P(('grp', 'dev')), may hold values from -0.375 to 0.375
- decoder: bfloat16 [524288, 256], P(('grp', 'dev')), may hold values from -0.375 to 0.375
Outputs:
- target_values: bfloat16 [524288, 768], P(('grp', 'dev'))
All inputs are finite; a program needn't handle non-finite values.
Results may differ from a plain program's by a relative error of at most 0.02.
Values may be sent and summed in bfloat16 or wider, within the bound.
A program may use at most 64 MiB of HBM per device.

v0:
```python
import jax
import jax.numpy as jnp
from jax import lax
from jax.sharding import Mesh
from jax.sharding import PartitionSpec as P

K = 256
LOCAL = 3
GRP = ("grp_0", "grp_1")
GRP_DEV = ("grp_0", "grp_1", "dev")


def from_partner(block, axis, bit):
    count = lax.axis_size(axis)
    route = []
    for low in range(count):
        high = low | 1 << bit
        if high != low and high < count:
            route += [(low, high), (high, low)]
    return lax.ppermute(block, axis, route)


def gather_axes(x, axes, dim):
    result = x
    for number in range(len(axes) - 1, -1, -1):
        result = lax.all_gather(result, axes[number], axis=dim, tiled=True)
    return result


def shards(sources, encoder, section_weight, cross_weight, local_weight, decoder):
    coeffs = lax.dot_general(
        encoder, sources, (((0,), (0,)), ((), ())), preferred_element_type=jnp.float32
    ).astype(jnp.bfloat16)
    section_count = lax.axis_size("dev").bit_length() - 1
    for section_bit in range(section_count):
        partner = from_partner(coeffs, "dev", section_bit)
        keep_matrix = section_weight[0, section_bit, 0]
        take_matrix = section_weight[0, section_bit, 1]
        coeffs = (
            jnp.dot(keep_matrix, coeffs, preferred_element_type=jnp.float32)
            + jnp.dot(take_matrix, partner, preferred_element_type=jnp.float32)
        ).astype(jnp.bfloat16)
    own_cross = cross_weight[0, 0]
    merged = jnp.einsum(
        "hkl,hlr->kr",
        own_cross,
        gather_axes(coeffs[None], GRP, 0),
        preferred_element_type=jnp.float32,
    ).astype(jnp.bfloat16)
    blocks = merged[None]
    offset = 0
    for depth_level in range(LOCAL):
        children = 2 ** (depth_level + 1)
        matrices = local_weight[0, offset : offset + children].reshape(children // 2, 2, K, K)
        blocks = jnp.einsum("jckl,jlr->jckr", matrices, blocks, preferred_element_type=jnp.float32)
        blocks = blocks.reshape(children, K, blocks.shape[-1]).astype(jnp.bfloat16)
        offset = offset + children
    decoder_leaves = decoder.reshape(2**LOCAL, -1, K)
    target_values = jnp.einsum(
        "ctk,ckr->ctr", decoder_leaves, blocks, preferred_element_type=jnp.float32
    )
    return target_values.reshape(-1, blocks.shape[-1]).astype(jnp.bfloat16)


def solution(mesh):
    torus = Mesh(mesh.devices.reshape(4, 2, mesh.shape["dev"]), ("grp_0", "grp_1", "dev"))
    placed = (
        P(GRP_DEV, None),
        P(GRP_DEV, None),
        P(GRP_DEV, None, None, None, None),
        P(GRP, "dev", None, None, None),
        P(GRP_DEV, None, None, None),
        P(GRP_DEV, None),
    )
    return jax.shard_map(
        shards, mesh=torus, in_specs=placed, out_specs=P(GRP_DEV, None), check_vma=False
    )
```

profile of v0, /device:TPU:54, one launch (start us, length us, event | category | flops | bytes accessed | tf_op | source)
XLA Modules:
  0.0 152.0 jit_solution(18093679877062004291)
XLA Ops:
  6.5 1.9 %copy-done = bf16[2048,768]{1,0:T(8,128)(2,1)S(1)} copy-done((bf16[2048,768]{1,0:T(8,128)(2,1)S(1)}, bf16[2048,768]{1,0:T(8,128)(2,1)}, u32[]{:S(2)}) %copy-start) | copy-done | bytes 3145752
  8.4 2.3 %convolution_convert_fusion.4 = bf16[256,768]{1,0:T(8,128)(2,1)S(1)} fusion(bf16[2048,256]{1,0:T(8,128)(2,1)} %param.7, bf16[2048,768]{1,0:T(8,128)(2,1)S(1)} %copy-done), kind=kOutput, calls=%fused_computation.17 | convolution fusion | flops 805502976 | bytes 4587520 | tf_op jit(solution)/shard_map/dot_general | solution.py:31
  10.9 0.3 fusion.27
  11.2 1.4 collective-permute-done
  12.6 0.3 fusion.1
  13.4 10.8 %collective-permute-done.1 = bf16[256,768]{0,1:T(8,128)(2,1)S(1)} collective-permute-done((bf16[256,768]{0,1:T(8,128)(2,1)S(1)}, bf16[256,768]{0,1:T(8,128)(2,1)S(1)}, u32[]{:S(2)}, u32[]{:S(2)}) %collective-permute-start.1) | collective-permute-done | bytes 393248 | tf_op jit(solution)/shard_map/ppermute | solution.py:20
  24.4 3.4 %collective-permute-start.2 = (bf16[256,768]{0,1:T(8,128)(2,1)S(1)}, bf16[256,768]{0,1:T(8,128)(2,1)S(1)}, u32[]{:S(2)}, u32[]{:S(2)}) collective-permute-start(bf16[256,768]{0,1:T(8,128)(2,1)S(1)} %bitcast.101), channel_id=1, source_target_pairs={{0,4},{4,0},{1,5},{5,1},{2,6},{6,2},{3,7},{7,3},{8,12},{12,8},{9,1... | collective-permute-start | bytes 1179656 | tf_op jit(solution)/shard_map/ppermute | solution.py:20
  27.8 0.3 fusion.21
  28.1 15.8 %collective-permute-done.2 = bf16[256,768]{0,1:T(8,128)(2,1)S(1)} collective-permute-done((bf16[256,768]{0,1:T(8,128)(2,1)S(1)}, bf16[256,768]{0,1:T(8,128)(2,1)S(1)}, u32[]{:S(2)}, u32[]{:S(2)}) %collective-permute-start.2) | collective-permute-done | bytes 393248 | tf_op jit(solution)/shard_map/ppermute | solution.py:20
  44.0 0.3 fusion.3
  44.2 0.9 collective-permute-start.3
  45.5 9.9 %collective-permute-done.3 = bf16[256,768]{0,1:T(8,128)(2,1)S(1)} collective-permute-done((bf16[256,768]{0,1:T(8,128)(2,1)S(1)}, bf16[256,768]{0,1:T(8,128)(2,1)S(1)}, u32[]{:S(2)}, u32[]{:S(2)}) %collective-permute-start.3) | collective-permute-done | bytes 393248 | tf_op jit(solution)/shard_map/ppermute | solution.py:20
  55.7 1.5 collective-permute-start.4
  57.2 0.3 fusion.15
  57.5 10.0 %collective-permute-done.4 = bf16[256,768]{0,1:T(8,128)(2,1)S(1)} collective-permute-done((bf16[256,768]{0,1:T(8,128)(2,1)S(1)}, bf16[256,768]{0,1:T(8,128)(2,1)S(1)}, u32[]{:S(2)}, u32[]{:S(2)}) %collective-permute-start.4) | collective-permute-done | bytes 393248 | tf_op jit(solution)/shard_map/ppermute | solution.py:20
  67.8 14.1 %all-gather = bf16[512,768]{0,1:T(8,128)(2,1)} all-gather(bf16[256,768]{0,1:T(8,128)(2,1)S(1)} %fusion.8), channel_id=2, replica_groups=mesh['grp_0'=4,'grp_1'=2,'dev'=32] {'grp_1'}, dimensions={0}, use_global_device_ids=true | all-gather | bytes 1179648 | tf_op jit(solution)/shard_map/all_gather | solution.py:26
  81.9 2.3 %copy.13 = bf16[512,768]{1,0:T(8,128)(2,1)} copy(bf16[512,768]{0,1:T(8,128)(2,1)} %all-gather) | data formatting | bytes 1572864 | tf_op jit(solution)/shard_map/all_gather | solution.py:26
  84.2 1.9 %slice.50 = bf16[1,4,256,256]{3,2,1,0:T(8,128)(2,1)} slice(bf16[1,14,256,256]{3,2,1,0:T(8,128)(2,1)} %param.10), slice={[0:1], [2:6], [0:256], [0:256]} | slice | bytes 1048576 | tf_op jit(solution)/shard_map/slice | solution.py:54
  86.1 2.3 %slice.51 = bf16[1,8,256,256]{3,2,1,0:T(8,128)(2,1)} slice(bf16[1,14,256,256]{3,2,1,0:T(8,128)(2,1)} %param.10), slice={[0:1], [6:14], [0:256], [0:256]} | slice | bytes 2097152 | tf_op jit(solution)/shard_map/slice | solution.py:54
  88.4 45.0 %all-gather.3.cloned.1.call-done = bf16[8,256,768]{2,1,0:T(8,128)(2,1)} async-done(((bf16[2,256,768]{2,1,0:T(8,128)(2,1)}), bf16[8,256,768]{2,1,0:T(8,128)(2,1)}) %all-gather.3.cloned.1.call-update) | async-done | bytes 3145744 | tf_op jit(solution)/shard_map/all_gather | solution.py:26
  133.4 3.2 %fusion.7 = bf16[768,256,1]{1,0,2:T(8,128)(2,1)S(1)} fusion(bf16[8,256,768]{2,1,0:T(8,128)(2,1)} %all-gather.3.cloned.1.call-done, bf16[1,1,8,256,256]{4,3,2,1,0:T(8,128)(2,1)} %param.9), kind=kOutput, calls=%fused_computation.18 | convolution fusion | flops 805502976 | bytes 4587520 | tf_op jit(solution)/shard_map/hkl,hlr->kr/dot_general | solution.py:44
  136.6 3.1 %convolution_convert_fusion.2 = bf16[2,768,2,256]{3,1,2,0:T(8,128)(2,1)} fusion(bf16[2,2,256,256]{3,2,1,0:T(8,128)(2,1)} %bitcast.99, bf16[768,256,1]{1,0,2:T(8,128)(2,1)S(1)} %fusion.7, bf16[1,14,256,256]{3,2,1,0:T(8,128)(2,1)} %param.10), kind=kOutput, calls=%fused_computation.2 | convolution fusion | flops 605159424 | bytes 2752512 | tf_op jit(solution)/shard_map/jckl,jlr->jckr/dot_general | solution.py:55
  139.7 2.8 %convolution_convert_fusion.1 = bf16[4,768,2,256]{3,1,2,0:T(8,128)(2,1)S(1)} fusion(bf16[4,256,768,1]{1,2,3,0:T(8,128)(2,1)} %bitcast.96, bf16[4,2,256,256]{3,2,1,0:T(8,128)(2,1)} %bitcast.97), kind=kOutput, calls=%fused_computation.1 | convolution fusion | flops 806879232 | bytes 5767168 | tf_op jit(solution)/shard_map/jckl,jlr->jckr/dot_general | solution.py:55
  142.5 2.7 %convolution_convert_fusion = bf16[8,768,256]{1,2,0:T(8,128)(2,1)} fusion(bf16[8,256,768]{1,2,0:T(8,128)(2,1)S(1)} %bitcast.95, bf16[8,256,256]{2,1,0:T(8,128)(2,1)S(1)} %bitcast.104), kind=kOutput, calls=%fused_computation | convolution fusion | flops 806879232 | bytes 7340032 | tf_op jit(solution)/shard_map/ctk,ckr->ctr/dot_general | solution.py:59
  (14 shorter events, 1.8 us)
Async XLA Ops:
  6.5 1.9 %copy-start = (bf16[2048,768]{1,0:T(8,128)(2,1)S(1)}, bf16[2048,768]{1,0:T(8,128)(2,1)}, u32[]{:S(2)}) copy-start(bf16[2048,768]{1,0:T(8,128)(2,1)} %param.6) | copy-start | bytes 9437188
  6.5 126.8 %all-gather.3.cloned.1.call-start = ((), (), s32[]{:S(2)}) async-start(), calls=%async_computation | async-start | bytes 3932160 | tf_op jit(solution)/shard_map/all_gather | solution.py:26
  8.4 2.4 %copy-start.1 = (bf16[1,5,2,256,256]{4,3,2,1,0:T(8,128)(2,1)S(1)}, bf16[1,5,2,256,256]{4,3,2,1,0:T(8,128)(2,1)}, u32[]{:S(2)}) copy-start(bf16[1,5,2,256,256]{4,3,2,1,0:T(8,128)(2,1)} %param.8) | copy-start | bytes 3932164
  10.8 1.8 %collective-permute-start = (bf16[256,768]{1,0:T(8,128)(2,1)S(1)}, bf16[256,768]{1,0:T(8,128)(2,1)S(1)}, u32[]{:S(2)}, u32[]{:S(2)}) collective-permute-start(bf16[256,768]{1,0:T(8,128)(2,1)S(1)} %convolution_convert_fusion.4), channel_id=1, source_target_pairs={{0,1},{1,0},{2,3},{3,2},{4,5},{5,4},{6,7},{7,6},{8,9},{9,8},{10,11... | collective-permute-start | bytes 1179656 | tf_op jit(solution)/shard_map/ppermute | solution.py:20
  12.9 11.2 %collective-permute-start.1 = (bf16[256,768]{0,1:T(8,128)(2,1)S(1)}, bf16[256,768]{0,1:T(8,128)(2,1)S(1)}, u32[]{:S(2)}, u32[]{:S(2)}) collective-permute-start(bf16[256,768]{0,1:T(8,128)(2,1)S(1)} %bitcast.100), channel_id=1, source_target_pairs={{0,2},{2,0},{1,3},{3,1},{4,6},{6,4},{5,7},{7,5},{8,10},{10,8},{9,1... | collective-permute-start | bytes 1179656 | tf_op jit(solution)/shard_map/ppermute | solution.py:20
  24.4 19.5 %collective-permute-start.2 = (bf16[256,768]{0,1:T(8,128)(2,1)S(1)}, bf16[256,768]{0,1:T(8,128)(2,1)S(1)}, u32[]{:S(2)}, u32[]{:S(2)}) collective-permute-start(bf16[256,768]{0,1:T(8,128)(2,1)S(1)} %bitcast.101), channel_id=1, source_target_pairs={{0,4},{4,0},{1,5},{5,1},{2,6},{6,2},{3,7},{7,3},{8,12},{12,8},{9,1... | collective-permute-start | bytes 1179656 | tf_op jit(solution)/shard_map/ppermute | solution.py:20
  44.2 11.1 %collective-permute-start.3 = (bf16[256,768]{0,1:T(8,128)(2,1)S(1)}, bf16[256,768]{0,1:T(8,128)(2,1)S(1)}, u32[]{:S(2)}, u32[]{:S(2)}) collective-permute-start(bf16[256,768]{0,1:T(8,128)(2,1)S(1)} %bitcast.102), channel_id=1, source_target_pairs={{0,8},{8,0},{1,9},{9,1},{2,10},{10,2},{3,11},{11,3},{4,12},{12,4},... | collective-permute-start | bytes 1179656 | tf_op jit(solution)/shard_map/ppermute | solution.py:20
  55.7 11.8 %collective-permute-start.4 = (bf16[256,768]{0,1:T(8,128)(2,1)S(1)}, bf16[256,768]{0,1:T(8,128)(2,1)S(1)}, u32[]{:S(2)}, u32[]{:S(2)}) collective-permute-start(bf16[256,768]{0,1:T(8,128)(2,1)S(1)} %bitcast.103), channel_id=1, source_target_pairs={{0,16},{16,0},{1,17},{17,1},{2,18},{18,2},{3,19},{19,3},{4,20},{20... | collective-permute-start | bytes 1179656 | tf_op jit(solution)/shard_map/ppermute | solution.py:20
  139.7 2.8 %copy-start.2 = (bf16[2048,256]{1,0:T(8,128)(2,1)S(1)}, bf16[2048,256]{1,0:T(8,128)(2,1)}, u32[]{:S(2)}) copy-start(bf16[2048,256]{1,0:T(8,128)(2,1)} %param.11) | copy-start | bytes 3145732
Sparse Core Ops, SparseCore 0:
  84.3 49.0 all-gather.2
where the time goes:
time: 155 us; the launch traced here: 152 us
  waiting for transfers between devices  92.9 us (60%)
  matrix products  17 us (11%)
  blocking collectives  14.1 us (9%)
  between operations  13.5 us (9%)
  local copies, waits for them, and re-layouts  8.34 us (5%)
  starting transfers between devices  6.06 us (4%)
    ppermute x5, waiting for transfers between devices, from_partner(): return lax.ppermute(block, axis, route)  47.9 us
    all_gather x1, waiting for transfers between devices, gather_axes(): result = lax.all_gather(result, axes[number], axis=dim, tiled=True)  45 us
    all_gather x1, blocking collectives, gather_axes(): result = lax.all_gather(result, axes[number], axis=dim, tiled=True)  14.1 us
    ppermute x5, starting transfers between devices, from_partner(): return lax.ppermute(block, axis, route)  6.06 us
    dot_general x2, matrix products, shards(): jnp.einsum('jckl,jlr->jckr', matrices, blocks, preferred_element_type=jnp...  5.88 us
    slice x2, local copies, waits for them, and re-layouts, shards(): local_weight[0, offset:offset + children].reshape(children // 2, 2, K, K)  4.16 us
    dot_general x1, matrix products, shards(): jnp.einsum('hkl,hlr->kr', own_cross, gather_axes(coeffs[None], GRP, 0), p...  3.19 us
  transfers between devices with their start and end apart: 6, of which 6 were waited for; matrix products, arithmetic and copies ran while one was open for 4% of the time, Pallas kernels for 0%

commit v1 on v0

v1 whole, which is shorter than its diff:
```python
import math

import jax
import jax.numpy as jnp
from jax import lax
from jax.experimental import pallas as pl
from jax.experimental.pallas import tpu as pltpu
from jax.sharding import PartitionSpec as P

K = 256
LOCAL = 3
SECTIONS = 5
GROUPS = 8
WIDTH = 128
MESH = pl.DeviceIdType.MESH

TIMES = {
    "encode": 0.0,
    "section0": 0.45,
    "section1": 1.6,
    "section2": 3.4,
    "section3": 4.5,
    "section4": 5.7,
    "relay": 6.8,
    "spread": 8.2,
    "relay_far": 9.3,
    "finish": 10.3,
}

OWN, BELOW, ABOVE, ACROSS, FAR, FAR_BELOW, FAR_ABOVE, FAR_ACROSS = range(GROUPS)
(TO_BELOW, TO_ABOVE, TO_ACROSS_UP, TO_ACROSS_DOWN, TO_FAR,
 TO_FAR_BELOW, TO_FAR_ABOVE, TO_FAR_ACROSS_UP, TO_FAR_ACROSS_DOWN) = range(SECTIONS, SECTIONS + 9)
COPIES = SECTIONS + 9


def flip(index, bit):
    size = 2**bit
    return index + size - 2 * size * lax.rem(lax.div(index, size), 2)


def kernel(sources, encoder, section_weight, cross_weight, local_weight, decoder, target,
           src, enc, enc_t, pair_w, cross_w, local_w, dec, pairs, gathered, blocks, out,
           load_sem, src_sem, out_sem, send_sem, recv_sem):
    chunks = src.shape[0]
    grp, dev = lax.axis_index("grp"), lax.axis_index("dev")
    height = lax.div(grp, 2)
    half = lax.rem(grp, 2)

    def group(step, far):
        return 2 * lax.rem(height + step, 4) + (1 - half if far else half)

    partners = [(grp, flip(dev, bit)) for bit in range(SECTIONS)]
    below, above, far = (group(3, False), dev), (group(1, False), dev), (group(0, True), dev)

    barrier = pltpu.get_barrier_semaphore()
    for device in (*partners, below, above, far):
        pl.semaphore_signal(barrier, inc=1, device_id=device, device_id_type=MESH)

    def load_sources(j):
        return pltpu.make_async_copy(
            sources.at[:, pl.ds(pl.multiple_of(j * WIDTH, WIDTH), WIDTH)], src.at[j], src_sem.at[j]
        )

    loads = {"encoder": [(encoder, enc)]}
    for bit in range(SECTIONS):
        loads[f"section{bit}"] = [
            (section_weight.at[0, bit, side], pair_w.at[bit, :, pl.ds(side * K, K)]) for side in range(2)
        ]
    order = [group(step, away) for away in (False, True) for step in (0, 3, 1, 2)]
    loads["cross"] = [
        (cross_weight.at[0, 0, order[slot]], cross_w.at[:, pl.ds(slot * K, K)]) for slot in range(GROUPS)
    ]
    loads["local"] = [(local_weight.at[0], local_w)]
    loads["decoder"] = [(decoder, dec)]
    copies, number = {}, 0
    for name, moves in loads.items():
        copies[name] = []
        for start, end in moves:
            copies[name].append(pltpu.make_async_copy(start, end, load_sem.at[number]))
            number += 1

    def begin(name):
        for copy in copies[name]:
            copy.start()

    def ready(name):
        for copy in copies[name]:
            copy.wait()

    begin("encoder")
    load_sources(0).start()
    begin("section0")
    for j in range(1, chunks):
        load_sources(j).start()
    for bit in range(1, SECTIONS):
        begin(f"section{bit}")
    begin("cross")
    begin("local")
    begin("decoder")

    ready("encoder")
    for block in range(enc.shape[0] // K):
        rows = pl.ds(block * K, K)
        enc_t[:, rows] = enc[rows, :].T
    pl.semaphore_wait(barrier, 8)

    def copy(kind, j, start, end, device):
        return pltpu.make_async_remote_copy(
            src_ref=start, dst_ref=end, send_sem=send_sem.at[kind, j], recv_sem=recv_sem.at[kind, j],
            device_id=device, device_id_type=MESH,
        )

    def slot(j, number, first=0, rows=K):
        return gathered.at[j, pl.ds(number * K + first, rows)]

    def exchange(bit, j):
        return copy(bit, j, pairs.at[bit, j, pl.ds(0, K)], pairs.at[bit, j, pl.ds(K, K)], partners[bit])

    def gather(kind, j):
        upper, lower = (0, K // 2), (K // 2, K // 2)
        start, end, device = {
            TO_ABOVE: (slot(j, OWN), slot(j, BELOW), above),
            TO_BELOW: (slot(j, OWN), slot(j, ABOVE), below),
            TO_ACROSS_UP: (slot(j, BELOW, *upper), slot(j, ACROSS, *upper), above),
            TO_ACROSS_DOWN: (slot(j, ABOVE, *lower), slot(j, ACROSS, *lower), below),
            TO_FAR: (slot(j, OWN), slot(j, FAR), far),
            TO_FAR_ABOVE: (slot(j, FAR), slot(j, FAR_BELOW), above),
            TO_FAR_BELOW: (slot(j, FAR), slot(j, FAR_ABOVE), below),
            TO_FAR_ACROSS_UP: (slot(j, FAR_BELOW, *upper), slot(j, FAR_ACROSS, *upper), above),
            TO_FAR_ACROSS_DOWN: (slot(j, FAR_ABOVE, *lower), slot(j, FAR_ACROSS, *lower), below),
        }[kind]
        return copy(kind, j, start, end, device)

    def result(j):
        return pltpu.make_async_copy(
            out.at[j], target.at[:, pl.ds(pl.multiple_of(j * WIDTH, WIDTH), WIDTH)], out_sem.at[j]
        )

    def dot(a, b):
        return jnp.dot(a, b, preferred_element_type=jnp.float32).astype(jnp.bfloat16)

    def encode(j):
        load_sources(j).wait()
        pairs[0, j, 0:K] = dot(enc_t[...], src[j])
        exchange(0, j).start()

    def section(bit, j):
        pl.when(j == 0)(lambda: ready(f"section{bit}"))
        exchange(bit, j).wait_recv()
        mixed = dot(pair_w[bit], pairs[bit, j])
        if bit + 1 < SECTIONS:
            pairs[bit + 1, j, 0:K] = mixed
            exchange(bit + 1, j).start()
        else:
            gathered[j, 0:K] = mixed
            for kind in (TO_FAR, TO_ABOVE, TO_BELOW):
                gather(kind, j).start()

    def relay(j):
        gather(TO_ABOVE, j).wait_recv()
        gather(TO_ACROSS_UP, j).start()
        gather(TO_BELOW, j).wait_recv()
        gather(TO_ACROSS_DOWN, j).start()

    def spread(j):
        gather(TO_FAR, j).wait_recv()
        gather(TO_FAR_ABOVE, j).start()
        gather(TO_FAR_BELOW, j).start()

    def relay_far(j):
        gather(TO_FAR_ABOVE, j).wait_recv()
        gather(TO_FAR_ACROSS_UP, j).start()
        gather(TO_FAR_BELOW, j).wait_recv()
        gather(TO_FAR_ACROSS_DOWN, j).start()

    def finish(j):
        @pl.when(j == 0)
        def _():
            ready("cross")
            ready("local")
            ready("decoder")

        for kind in (TO_ACROSS_UP, TO_ACROSS_DOWN, TO_FAR_ACROSS_UP, TO_FAR_ACROSS_DOWN):
            gather(kind, j).wait_recv()
        blocks[0, 0:K] = dot(cross_w[...], gathered[j])
        offset = 0
        for level in range(LOCAL):
            for parent in range(2**level):
                rows = slice(2 * parent * K, 2 * (parent + 1) * K)
                blocks[level + 1, rows] = dot(
                    local_w[offset + rows.start : offset + rows.stop], blocks[level, parent * K : (parent + 1) * K]
                )
            offset += 2 ** (level + 1) * K
        leaf = dec.shape[0] // 2**LOCAL
        for child in range(2**LOCAL):
            rows = slice(child * leaf, (child + 1) * leaf)
            out[j, rows] = dot(dec[rows], blocks[LOCAL, child * K : (child + 1) * K])
        result(j).start()

    tasks = {"encode": encode, "relay": relay, "spread": spread, "relay_far": relay_far, "finish": finish}
    for bit in range(SECTIONS):
        tasks[f"section{bit}"] = lambda j, bit=bit: section(bit, j)
    body = sorted(TIMES, key=lambda name: TIMES[name] % 1)
    last = max(math.floor(time) for time in TIMES.values())

    def step(t, carry):
        for name in body:
            j = t - math.floor(TIMES[name])
            pl.when((j >= 0) & (j < chunks))(lambda name=name, j=j: tasks[name](j))
        return carry

    lax.fori_loop(0, chunks + last, step, 0)

    def drain(j, carry):
        for bit in range(SECTIONS):
            exchange(bit, j).wait_send()
        for kind in range(SECTIONS, COPIES):
            gather(kind, j).wait_send()
        result(j).wait()
        return carry

    lax.fori_loop(0, chunks, drain, 0)


def shards(sources, encoder, section_weight, cross_weight, local_weight, decoder):
    points, columns = sources.shape
    chunks = columns // WIDTH
    matrices = local_weight.shape[1]
    bf16 = jnp.bfloat16
    anywhere = pl.BlockSpec(memory_space=pl.ANY)
    dma = pltpu.SemaphoreType.DMA
    return pl.pallas_call(
        kernel,
        out_shape=jax.ShapeDtypeStruct((decoder.shape[0], columns), bf16),
        in_specs=[anywhere] * 6,
        out_specs=anywhere,
        scratch_shapes=[
            pltpu.VMEM((chunks, points, WIDTH), bf16),
            pltpu.VMEM((points, K), bf16),
            pltpu.VMEM((K, points), bf16),
            pltpu.VMEM((SECTIONS, K, 2 * K), bf16),
            pltpu.VMEM((K, GROUPS * K), bf16),
            pltpu.VMEM((matrices * K, K), bf16),
            pltpu.VMEM(decoder.shape, bf16),
            pltpu.VMEM((SECTIONS, chunks, 2 * K, WIDTH), bf16),
            pltpu.VMEM((chunks, GROUPS * K, WIDTH), bf16),
            pltpu.VMEM((LOCAL + 1, 2**LOCAL * K, WIDTH), bf16),
            pltpu.VMEM((chunks, decoder.shape[0], WIDTH), bf16),
            dma((1 + 2 * SECTIONS + GROUPS + 2,)),
            dma((chunks,)),
            dma((chunks,)),
            dma((COPIES, chunks)),
            dma((COPIES, chunks)),
        ],
        compiler_params=pltpu.CompilerParams(
            collective_id=0, has_side_effects=True, vmem_limit_bytes=48 * 2**20
        ),
        name="butterfly",
    )(sources, encoder, section_weight, cross_weight, local_weight.reshape(1, matrices * K, K), decoder)


def solution(mesh):
    whole = ("grp", "dev")
    placed = (
        P(whole, None),
        P(whole, None),
        P(whole, None, None, None, None),
        P("grp", "dev", None, None, None),
        P(whole, None, None, None),
        P(whole, None),
    )
    return jax.shard_map(shards, mesh=mesh, in_specs=placed, out_specs=P(whole, None), check_vma=False)
```

time: 155 us -> 86 us (0.55)
  the two profiles are of different devices: /device:TPU:54 before, /device:TPU:8 now
where the time goes in v1:
time: 86 us; the launch traced here: 85.8 us
  Pallas kernels  77 us (90%)
  local copies, waits for them, and re-layouts  8.74 us (10%)
    pallas_call x1, Pallas kernels, shards(): pl.pallas_call(kernel, out_shape=jax.ShapeDtypeStruct((decoder.shape[0],...  77 us
    unnamed x9, local copies, waits for them, and re-layouts  8.74 us

profile of v1, /device:TPU:8, one launch (start us, length us, event | category | flops | bytes accessed | tf_op | source)
XLA Modules:
  0.0 85.8 jit_solution(13357967918415497231)
XLA Ops:
  0.0 0.0 copy-start
  0.0 1.3 %copy-done = bf16[1,5,2,256,256]{4,3,2,1,0:T(8,128)(2,1)S(1)} copy-done((bf16[1,5,2,256,256]{4,3,2,1,0:T(8,128)(2,1)S(1)}, bf16[1,5,2,256,256]{4,3,2,1,0:T(8,128)(2,1)}, u32[]{:S(2)}) %copy-start) | copy-done | bytes 1310744
  1.3 0.0 copy-start.1
  1.3 1.2 %copy-done.1 = bf16[2048,256]{1,0:T(8,128)(2,1)S(1)} copy-done((bf16[2048,256]{1,0:T(8,128)(2,1)S(1)}, bf16[2048,256]{1,0:T(8,128)(2,1)}, u32[]{:S(2)}) %copy-start.1) | copy-done | bytes 1048600
  2.5 0.0 copy-start.2
  2.5 1.2 %copy-done.2 = bf16[1,1,8,256,256]{4,3,2,1,0:T(8,128)(2,1)S(1)} copy-done((bf16[1,1,8,256,256]{4,3,2,1,0:T(8,128)(2,1)S(1)}, bf16[1,1,8,256,256]{4,3,2,1,0:T(8,128)(2,1)}, u32[]{:S(2)}) %copy-start.2) | copy-done | bytes 1048600
  3.8 0.0 copy-start.3
  3.8 1.2 %copy-done.3 = bf16[2048,256]{1,0:T(8,128)(2,1)S(1)} copy-done((bf16[2048,256]{1,0:T(8,128)(2,1)S(1)}, bf16[2048,256]{1,0:T(8,128)(2,1)}, u32[]{:S(2)}) %copy-start.3) | copy-done | bytes 1048600
  5.0 77.0 %butterfly.1 = bf16[2048,768]{1,0:T(8,128)(2,1)} custom-call(bf16[2048,768]{1,0:T(8,128)(2,1)} %sources.1, bf16[2048,256]{1,0:T(8,128)(2,1)S(1)} %copy-done.1, bf16[1,5,2,256,256]{4,3,2,1,0:T(8,128)(2,1)S(1)} %copy-done, bf16[1,1,8,256,256]{4,3,2,1,0:T(8,128)(2,1)S(1)} %copy-done.2, bf16[1,3584,256]{2,1,0:T(8,128)(2,1)} %bitcast.1, ...), custom_call_target="tpu_custom_call" | custom-call | tf_op jit(solution)/shard_map/butterfly/pallas_call | solution.py:232
  82.0 3.8 %copy.8 = bf16[2048,768]{1,0:T(8,128)(2,1)} copy(bf16[2048,768]{1,0:T(8,128)(2,1)} %butterfly.1) | data formatting | bytes 6291456
Async XLA Ops:
  0.0 1.3 %copy-start = (bf16[1,5,2,256,256]{4,3,2,1,0:T(8,128)(2,1)S(1)}, bf16[1,5,2,256,256]{4,3,2,1,0:T(8,128)(2,1)}, u32[]{:S(2)}) copy-start(bf16[1,5,2,256,256]{4,3,2,1,0:T(8,128)(2,1)} %section_weight.1) | copy-start | bytes 3932164
  1.3 1.2 %copy-start.1 = (bf16[2048,256]{1,0:T(8,128)(2,1)S(1)}, bf16[2048,256]{1,0:T(8,128)(2,1)}, u32[]{:S(2)}) copy-start(bf16[2048,256]{1,0:T(8,128)(2,1)} %encoder.1) | copy-start | bytes 3145732
  2.5 1.2 %copy-start.2 = (bf16[1,1,8,256,256]{4,3,2,1,0:T(8,128)(2,1)S(1)}, bf16[1,1,8,256,256]{4,3,2,1,0:T(8,128)(2,1)}, u32[]{:S(2)}) copy-start(bf16[1,1,8,256,256]{4,3,2,1,0:T(8,128)(2,1)} %cross_weight.1) | copy-start | bytes 3145732
  3.8 1.2 %copy-start.3 = (bf16[2048,256]{1,0:T(8,128)(2,1)S(1)}, bf16[2048,256]{1,0:T(8,128)(2,1)}, u32[]{:S(2)}) copy-start(bf16[2048,256]{1,0:T(8,128)(2,1)} %decoder.1) | copy-start | bytes 3145732

commit v2 on v1

v2 whole, which is shorter than its diff:
```python
import math

import jax
import jax.numpy as jnp
from jax import lax
from jax.experimental import pallas as pl
from jax.experimental.pallas import tpu as pltpu
from jax.sharding import PartitionSpec as P

K = 256
LOCAL = 3
SECTIONS = 5
WIDTH = 128
HELD = 3
MESH = pl.DeviceIdType.MESH

TIMES = {
    "encode": 0.0,
    "section0": 0.45,
    "section1": 1.6,
    "section2": 3.4,
    "section3": 4.5,
    "section4": 5.7,
    "release": 8.41,
    "spread": 10.2,
    "mix": 12.3,
    "finish": 14.4,
}

OWN, PAIR, FAR, FAR_PAIR = range(4)
NEAR = 4
TO_PAIR, TO_FAR, FAR_TO_PAIR, PARTIAL = range(SECTIONS, SECTIONS + 4)
COPIES = SECTIONS + 4


def flip(index, bit):
    size = 2**bit
    return index + size - 2 * size * lax.rem(lax.div(index, size), 2)


def kernel(sources, encoder, section_weight, cross_weight, local_weight, leaves,
           src, enc, enc_t, pair_w, cross_w, local_w, pairs, gathered, sums, partial, blocks,
           load_sem, src_sem, out_sem, send_sem, recv_sem, give_sem, take_sem):
    chunks = src.shape[0]
    grp, dev = lax.axis_index("grp"), lax.axis_index("dev")
    height = lax.div(grp, 2)
    half = lax.rem(grp, 2)

    heights = [height + 1 - 2 * lax.rem(height, 2), lax.rem(height + 3 + 2 * lax.rem(height, 2), 4)]
    across = lax.rem(height + 2, 4)
    beside = [2 * place + half for place in heights]

    partners = [(grp, flip(dev, bit)) for bit in range(SECTIONS)]
    far = (grp + 1 - 2 * half, dev)

    barrier = pltpu.get_barrier_semaphore()
    for device in (*partners, (beside[0], dev), (beside[1], dev), far):
        pl.semaphore_signal(barrier, inc=1, device_id=device, device_id_type=MESH)

    def load_sources(j):
        return pltpu.make_async_copy(
            sources.at[:, pl.ds(pl.multiple_of(j * WIDTH, WIDTH), WIDTH)], src.at[j], src_sem.at[j]
        )

    loads = {"encoder": [(encoder, enc)]}
    for bit in range(SECTIONS):
        loads[f"section{bit}"] = [
            (section_weight.at[0, bit, side], pair_w.at[bit, :, pl.ds(side * K, K)]) for side in range(2)
        ]
    def matrix(place, away):
        return cross_weight.at[0, 0, 2 * place + (1 - half if away else half)]

    def columns(slot):
        return pl.ds(slot * K, K)

    loads["cross"], gifts = [], []
    for turn in range(2):
        for slot, place in ((OWN, height), (PAIR, heights[turn]), (FAR, height), (FAR_PAIR, heights[turn])):
            loads["cross"].append((matrix(place, slot >= FAR), cross_w.at[turn, pl.ds(0, K), columns(slot)]))
        for slot, place in ((OWN, heights[1 - turn]), (PAIR, across), (FAR, heights[1 - turn]), (FAR_PAIR, across)):
            gifts.append(pltpu.make_async_remote_copy(
                src_ref=matrix(place, slot >= FAR), dst_ref=cross_w.at[turn, pl.ds(K, K), columns(slot)],
                send_sem=give_sem.at[turn, slot], recv_sem=take_sem.at[turn, slot],
                device_id=(beside[1 - turn], dev), device_id_type=MESH,
            ))
    loads["local"] = [(local_weight.at[0], local_w)]
    copies, number = {}, 0
    for name, moves in loads.items():
        copies[name] = []
        for start, end in moves:
            copies[name].append(pltpu.make_async_copy(start, end, load_sem.at[number]))
            number += 1

    def begin(name):
        for copy in copies[name]:
            copy.start()

    def ready(name):
        for copy in copies[name]:
            copy.wait()

    begin("encoder")
    load_sources(0).start()
    ready("encoder")
    for block in range(enc.shape[0] // K):
        rows = pl.ds(block * K, K)
        enc_t[:, rows] = enc[rows, :].T
    load_sources(0).wait()
    begin("section0")
    load_sources(1).start()
    begin("section1")
    for j in range(2, chunks):
        load_sources(j).start()
    for bit in range(2, SECTIONS):
        begin(f"section{bit}")
    begin("cross")
    begin("local")
    pl.semaphore_wait(barrier, 8)
    for gift in gifts:
        gift.start()

    def copy(kind, j, start, end, device):
        return pltpu.make_async_remote_copy(
            src_ref=start, dst_ref=end, send_sem=send_sem.at[kind, j], recv_sem=recv_sem.at[kind, j],
            device_id=device, device_id_type=MESH,
        )

    def slot(j, number):
        return gathered.at[j, pl.ds(number * K, K)]

    def exchange(bit, j):
        return copy(bit, j, pairs.at[bit, j, pl.ds(0, K)], pairs.at[bit, j, pl.ds(K, K)], partners[bit])

    def gather(kind, j):
        turn = lax.rem(j, 2)
        pair = (beside[0] + turn * (beside[1] - beside[0]), dev)
        other = (beside[1] + turn * (beside[0] - beside[1]), dev)
        start, end, device = {
            TO_PAIR: (slot(j, OWN), slot(j, PAIR), pair),
            TO_FAR: (slot(j, OWN), slot(j, FAR), far),
            FAR_TO_PAIR: (slot(j, FAR), slot(j, FAR_PAIR), pair),
            PARTIAL: (partial.at[0, j], partial.at[1, j], other),
        }[kind]
        return copy(kind, j, start, end, device)

    def result(j):
        return pltpu.make_async_copy(
            blocks.at[j, LOCAL], leaves.at[:, pl.ds(pl.multiple_of(j * WIDTH, WIDTH), WIDTH)], out_sem.at[j]
        )

    def dot32(a, b):
        return jnp.dot(a, b, preferred_element_type=jnp.float32)

    def dot(a, b):
        return dot32(a, b).astype(jnp.bfloat16)

    def encode(j):
        pl.when(j > 0)(lambda: load_sources(j).wait())
        pairs[0, j, 0:K] = dot(enc_t[...], src[j])
        exchange(0, j).start()

    def section(bit, j):
        pl.when(j == 0)(lambda: ready(f"section{bit}"))
        exchange(bit, j).wait_recv()
        mixed = dot(pair_w[bit], pairs[bit, j])
        if bit + 1 < SECTIONS:
            pairs[bit + 1, j, 0:K] = mixed
            exchange(bit + 1, j).start()
        else:
            gathered[j, 0:K] = mixed
            gather(TO_PAIR, j).start()

        if bit + 1 == SECTIONS:
            pl.when(j >= HELD)(lambda: gather(TO_FAR, j).start())

    def release(j):
        @pl.when(j == 0)
        def _():
            for held in range(HELD):
                gather(TO_FAR, held).start()

    def spread(j):
        gather(TO_FAR, j).wait_recv()
        gather(FAR_TO_PAIR, j).start()

    def mix(j):
        @pl.when(j == 0)
        def _():
            ready("cross")
            for gift in gifts:
                gift.wait_recv()

        gather(TO_PAIR, j).wait_recv()
        gather(FAR_TO_PAIR, j).wait_recv()
        both = dot32(cross_w[lax.rem(j, 2)], gathered[j])
        partial[0, j] = both[K:].astype(jnp.bfloat16)
        gather(PARTIAL, j).start()
        sums[j] = both[:K]

    def finish(j):
        @pl.when(j == 0)
        def _():
            ready("local")

        gather(PARTIAL, j).wait_recv()
        blocks[j, 0, 0:K] = (sums[j] + partial[1, j].astype(jnp.float32)).astype(jnp.bfloat16)
        offset = 0
        for level in range(LOCAL):
            for parent in range(2**level):
                rows = slice(2 * parent * K, 2 * (parent + 1) * K)
                blocks[j, level + 1, rows] = dot(
                    local_w[offset + rows.start : offset + rows.stop], blocks[j, level, parent * K : (parent + 1) * K]
                )
            offset += 2 ** (level + 1) * K
        result(j).start()

    tasks = {"encode": encode, "release": release, "spread": spread, "mix": mix, "finish": finish}
    for bit in range(SECTIONS):
        tasks[f"section{bit}"] = lambda j, bit=bit: section(bit, j)
    body = sorted(TIMES, key=lambda name: TIMES[name] % 1)
    last = max(math.floor(time) for time in TIMES.values())

    def step(t, carry):
        for name in body:
            j = t - math.floor(TIMES[name])
            pl.when((j >= 0) & (j < chunks))(lambda name=name, j=j: tasks[name](j))
        return carry

    lax.fori_loop(0, chunks + last, step, 0)

    def drain(j, carry):
        for bit in range(SECTIONS):
            exchange(bit, j).wait_send()
        for kind in range(SECTIONS, COPIES):
            gather(kind, j).wait_send()
        result(j).wait()
        return carry

    lax.fori_loop(0, chunks, drain, 0)
    for gift in gifts:
        gift.wait_send()


def decode(decoder, leaves, target, dec, leaf, out, dec_sem, leaf_sem, out_sem):
    count, rows, _ = dec.shape
    moves = []
    for c in range(count):
        span = pl.ds(c * rows, rows)
        moves.append((
            pltpu.make_async_copy(decoder.at[span], dec.at[c], dec_sem.at[c]),
            pltpu.make_async_copy(leaves.at[pl.ds(c * K, K)], leaf.at[c], leaf_sem.at[c]),
            pltpu.make_async_copy(out.at[c], target.at[span], out_sem.at[c]),
        ))
    for matrix, block, _ in moves:
        matrix.start()
        block.start()
    for c, (matrix, block, result) in enumerate(moves):
        matrix.wait()
        block.wait()
        out[c] = jnp.dot(dec[c], leaf[c], preferred_element_type=jnp.float32).astype(jnp.bfloat16)
        result.start()
    for *_, result in moves:
        result.wait()


def shards(sources, encoder, section_weight, cross_weight, local_weight, decoder):
    points, columns = sources.shape
    chunks = columns // WIDTH
    matrices = local_weight.shape[1]
    bf16 = jnp.bfloat16
    anywhere = pl.BlockSpec(memory_space=pl.ANY)
    dma = pltpu.SemaphoreType.DMA
    leaves = pl.pallas_call(
        kernel,
        out_shape=jax.ShapeDtypeStruct((2**LOCAL * K, columns), bf16),
        in_specs=[anywhere] * 5,
        out_specs=anywhere,
        scratch_shapes=[
            pltpu.VMEM((chunks, points, WIDTH), bf16),
            pltpu.VMEM((points, K), bf16),
            pltpu.VMEM((K, points), bf16),
            pltpu.VMEM((SECTIONS, K, 2 * K), bf16),
            pltpu.VMEM((2, 2 * K, NEAR * K), bf16),
            pltpu.VMEM((matrices * K, K), bf16),
            pltpu.VMEM((SECTIONS, chunks, 2 * K, WIDTH), bf16),
            pltpu.VMEM((chunks, NEAR * K, WIDTH), bf16),
            pltpu.VMEM((chunks, K, WIDTH), jnp.float32),
            pltpu.VMEM((2, chunks, K, WIDTH), bf16),
            pltpu.VMEM((chunks, LOCAL + 1, 2**LOCAL * K, WIDTH), bf16),
            dma((1 + 2 * SECTIONS + 2 * NEAR + 1,)),
            dma((chunks,)),
            dma((chunks,)),
            dma((COPIES, chunks)),
            dma((COPIES, chunks)),
            dma((2, NEAR)),
            dma((2, NEAR)),
        ],
        compiler_params=pltpu.CompilerParams(
            collective_id=0, has_side_effects=True, vmem_limit_bytes=62 * 2**20
        ),
        name="butterfly",
    )(sources, encoder, section_weight, cross_weight, local_weight.reshape(1, matrices * K, K))
    count = 2**LOCAL
    rows = decoder.shape[0] // count
    return pl.pallas_call(
        decode,
        out_shape=jax.ShapeDtypeStruct((decoder.shape[0], columns), bf16),
        in_specs=[anywhere] * 2,
        out_specs=anywhere,
        scratch_shapes=[
            pltpu.VMEM((count, rows, K), bf16),
            pltpu.VMEM((count, K, columns), bf16),
            pltpu.VMEM((count, rows, columns), bf16),
            dma((count,)),
            dma((count,)),
            dma((count,)),
        ],
        compiler_params=pltpu.CompilerParams(vmem_limit_bytes=62 * 2**20),
        name="decode",
    )(decoder, leaves)


def solution(mesh):
    whole = ("grp", "dev")
    placed = (
        P(whole, None),
        P(whole, None),
        P(whole, None, None, None, None),
        P("grp", "dev", None, None, None),
        P(whole, None, None, None),
        P(whole, None),
    )
    return jax.shard_map(shards, mesh=mesh, in_specs=placed, out_specs=P(whole, None), check_vma=False)
```

time: 86 us -> 69.6 us (0.81)
  the two profiles are of different devices: /device:TPU:8 before, /device:TPU:54 now
where the time goes in v2:
time: 69.6 us; the launch traced here: 69.5 us
  Pallas kernels  69.5 us (100%)
    pallas_call x1, Pallas kernels, shards(): pl.pallas_call(kernel, out_shape=jax.ShapeDtypeStruct((2 ** LOCAL * K, co...  65.1 us
    pallas_call x1, Pallas kernels, shards(): pl.pallas_call(decode, out_shape=jax.ShapeDtypeStruct((decoder.shape[0],...  4.45 us

profile of v2, /device:TPU:54, one launch (start us, length us, event | category | flops | bytes accessed | tf_op | source)
XLA Modules:
  0.0 69.5 jit_solution(2738806855495678237)
XLA Ops:
  0.0 65.1 %butterfly.1.leaves = bf16[2048,768]{1,0:T(8,128)(2,1)} custom-call(bf16[2048,768]{1,0:T(8,128)(2,1)} %sources.1, bf16[2048,256]{1,0:T(8,128)(2,1)} %encoder.1, bf16[1,5,2,256,256]{4,3,2,1,0:T(8,128)(2,1)} %section_weight.1, bf16[1,1,8,256,256]{4,3,2,1,0:T(8,128)(2,1)} %cross_weight.1, bf16[1,3584,256]{2,1,0:T(8,128)(2,1)} %bitcast.1), custom_call_target="tpu_custom_call" | custom-call | tf_op jit(solution)/shard_map/butterfly/pallas_call | solution.py:273
  65.1 4.4 %decode.1 = bf16[2048,768]{1,0:T(8,128)(2,1)} custom-call(bf16[2048,256]{1,0:T(8,128)(2,1)} %decoder.1, bf16[2048,768]{1,0:T(8,128)(2,1)} %butterfly.1.leaves), custom_call_target="tpu_custom_call" | custom-call | tf_op jit(solution)/shard_map/decode/pallas_call | solution.py:305

commit v3 on v2

--- a/solution.py
+++ b/solution.py
@@ -38,8 +38,8 @@
     return index + size - 2 * size * lax.rem(lax.div(index, size), 2)
 
 
-def kernel(sources, encoder, section_weight, cross_weight, local_weight, leaves,
-           src, enc, enc_t, pair_w, cross_w, local_w, pairs, gathered, sums, partial, blocks,
+def kernel(sources, encoder, section_weight, cross_weight, local_weight, decoder, leaves,
+           src, enc, enc_t, pair_w, cross_w, local_w, dec, pairs, gathered, sums, partial, blocks,
            load_sem, src_sem, out_sem, send_sem, recv_sem, give_sem, take_sem):
     chunks = src.shape[0]
     grp, dev = lax.axis_index("grp"), lax.axis_index("dev")
@@ -84,6 +84,7 @@
                 device_id=(beside[1 - turn], dev), device_id_type=MESH,
             ))
     loads["local"] = [(local_weight.at[0], local_w)]
+    loads["decoder"] = [(decoder, dec)]
     copies, number = {}, 0
     for name, moves in loads.items():
         copies[name] = []
@@ -115,6 +116,7 @@
         begin(f"section{bit}")
     begin("cross")
     begin("local")
+    begin("decoder")
     pl.semaphore_wait(barrier, 8)
     for gift in gifts:
         gift.start()
@@ -145,7 +147,7 @@
 
     def result(j):
         return pltpu.make_async_copy(
-            blocks.at[j, LOCAL], leaves.at[:, pl.ds(pl.multiple_of(j * WIDTH, WIDTH), WIDTH)], out_sem.at[j]
+            blocks.at[j, LOCAL + 1 - lax.div(j, chunks - 1)], leaves.at[:, pl.ds(pl.multiple_of(j * WIDTH, WIDTH), WIDTH)], out_sem.at[j]
         )
 
     def dot32(a, b):
@@ -201,6 +203,7 @@
         @pl.when(j == 0)
         def _():
             ready("local")
+            ready("decoder")
 
         gather(PARTIAL, j).wait_recv()
         blocks[j, 0, 0:K] = (sums[j] + partial[1, j].astype(jnp.float32)).astype(jnp.bfloat16)
@@ -212,6 +215,14 @@
                     local_w[offset + rows.start : offset + rows.stop], blocks[j, level, parent * K : (parent + 1) * K]
                 )
             offset += 2 ** (level + 1) * K
+
+        @pl.when(j < chunks - 1)
+        def _():
+            leaf = dec.shape[0] // 2**LOCAL
+            for child in range(2**LOCAL):
+                rows = slice(child * leaf, (child + 1) * leaf)
+                blocks[j, LOCAL + 1, rows] = dot(dec[rows], blocks[j, LOCAL, child * K : (child + 1) * K])
+
         result(j).start()
 
     tasks = {"encode": encode, "release": release, "spread": spread, "mix": mix, "finish": finish}
@@ -241,25 +252,25 @@
         gift.wait_send()
 
 
-def decode(decoder, leaves, target, dec, leaf, out, dec_sem, leaf_sem, out_sem):
-    count, rows, _ = dec.shape
+def decode(dec, leaves, target, leaf, leaf_sem, out_sem):
+    count, rows, columns = leaf.shape
+    last = pl.ds(columns - WIDTH, WIDTH)
     moves = []
     for c in range(count):
         span = pl.ds(c * rows, rows)
         moves.append((
-            pltpu.make_async_copy(decoder.at[span], dec.at[c], dec_sem.at[c]),
-            pltpu.make_async_copy(leaves.at[pl.ds(c * K, K)], leaf.at[c], leaf_sem.at[c]),
-            pltpu.make_async_copy(out.at[c], target.at[span], out_sem.at[c]),
+            pltpu.make_async_copy(leaves.at[span], leaf.at[c], leaf_sem.at[c]),
+            pltpu.make_async_copy(leaf.at[c], target.at[span], out_sem.at[c]),
         ))
-    for matrix, block, _ in moves:
-        matrix.start()
+    for block, _ in moves:
         block.start()
-    for c, (matrix, block, result) in enumerate(moves):
-        matrix.wait()
+    for c, (block, result) in enumerate(moves):
         block.wait()
-        out[c] = jnp.dot(dec[c], leaf[c], preferred_element_type=jnp.float32).astype(jnp.bfloat16)
+        leaf[c, :, last] = jnp.dot(
+            dec[c * rows : (c + 1) * rows], leaf[c, :, last], preferred_element_type=jnp.float32
+        ).astype(jnp.bfloat16)
         result.start()
-    for *_, result in moves:
+    for _, result in moves:
         result.wait()
 
 
@@ -273,7 +284,7 @@
     leaves = pl.pallas_call(
         kernel,
         out_shape=jax.ShapeDtypeStruct((2**LOCAL * K, columns), bf16),
-        in_specs=[anywhere] * 5,
+        in_specs=[anywhere] * 6,
         out_specs=anywhere,
         scratch_shapes=[
             pltpu.VMEM((chunks, points, WIDTH), bf16),
@@ -282,12 +293,13 @@
             pltpu.VMEM((SECTIONS, K, 2 * K), bf16),
             pltpu.VMEM((2, 2 * K, NEAR * K), bf16),
             pltpu.VMEM((matrices * K, K), bf16),
+            pltpu.VMEM(decoder.shape, bf16),
             pltpu.VMEM((SECTIONS, chunks, 2 * K, WIDTH), bf16),
             pltpu.VMEM((chunks, NEAR * K, WIDTH), bf16),
             pltpu.VMEM((chunks, K, WIDTH), jnp.float32),
             pltpu.VMEM((2, chunks, K, WIDTH), bf16),
-            pltpu.VMEM((chunks, LOCAL + 1, 2**LOCAL * K, WIDTH), bf16),
-            dma((1 + 2 * SECTIONS + 2 * NEAR + 1,)),
+            pltpu.VMEM((chunks, LOCAL + 2, 2**LOCAL * K, WIDTH), bf16),
+            dma((1 + 2 * SECTIONS + 2 * NEAR + 2,)),
             dma((chunks,)),
             dma((chunks,)),
             dma((COPIES, chunks)),
@@ -296,26 +308,24 @@
             dma((2, NEAR)),
         ],
         compiler_params=pltpu.CompilerParams(
-            collective_id=0, has_side_effects=True, vmem_limit_bytes=62 * 2**20
+            collective_id=0, has_side_effects=True, vmem_limit_bytes=60 * 2**20
         ),
         name="butterfly",
-    )(sources, encoder, section_weight, cross_weight, local_weight.reshape(1, matrices * K, K))
+    )(sources, encoder, section_weight, cross_weight, local_weight.reshape(1, matrices * K, K), decoder)
     count = 2**LOCAL
     rows = decoder.shape[0] // count
+    assert rows == K
     return pl.pallas_call(
         decode,
         out_shape=jax.ShapeDtypeStruct((decoder.shape[0], columns), bf16),
-        in_specs=[anywhere] * 2,
+        in_specs=[pl.BlockSpec(memory_space=pltpu.VMEM), anywhere],
         out_specs=anywhere,
         scratch_shapes=[
-            pltpu.VMEM((count, rows, K), bf16),
-            pltpu.VMEM((count, K, columns), bf16),
             pltpu.VMEM((count, rows, columns), bf16),
             dma((count,)),
             dma((count,)),
-            dma((count,)),
         ],
-        compiler_params=pltpu.CompilerParams(vmem_limit_bytes=62 * 2**20),
+        compiler_params=pltpu.CompilerParams(vmem_limit_bytes=50 * 2**20),
         name="decode",
     )(decoder, leaves)
 

time: 69.6 us -> 69.3 us (level)
    pallas_call x1, Pallas kernels: 4.45 us -> 3.5 us  [shards(): pl.pallas_call(decode, out_shape=jax.ShapeDtypeStruct((decoder.shape[0],...]
where the time goes in v3:
time: 69.3 us; the launch traced here: 69 us
  Pallas kernels  69 us (100%)
    pallas_call x1, Pallas kernels, shards(): pl.pallas_call(kernel, out_shape=jax.ShapeDtypeStruct((2 ** LOCAL * K, co...  65.5 us
    pallas_call x1, Pallas kernels, shards(): pl.pallas_call(decode, out_shape=jax.ShapeDtypeStruct((decoder.shape[0],...  3.5 us

profile of v3, /device:TPU:54, one launch (start us, length us, event | category | flops | bytes accessed | tf_op | source)
XLA Modules:
  0.0 69.0 jit_solution(13828790397389092527)
XLA Ops:
  0.0 0.0 copy-start
  0.0 65.5 %butterfly.1.leaves = bf16[2048,768]{1,0:T(8,128)(2,1)} custom-call(bf16[2048,768]{1,0:T(8,128)(2,1)} %sources.1, bf16[2048,256]{1,0:T(8,128)(2,1)} %encoder.1, bf16[1,5,2,256,256]{4,3,2,1,0:T(8,128)(2,1)} %section_weight.1, bf16[1,1,8,256,256]{4,3,2,1,0:T(8,128)(2,1)} %cross_weight.1, bf16[1,3584,256]{2,1,0:T(8,128)(2,1)} %bitcast.1, bf16[2048,256]{1,0:T(8,128)(2,1)} %dec.1), custom_call_target="tpu_custom_call" | custom-call | tf_op jit(solution)/shard_map/butterfly/pallas_call | solution.py:284
  65.5 0.0 copy-done
  65.5 3.5 %decode.1 = bf16[2048,768]{1,0:T(8,128)(2,1)} custom-call(bf16[2048,256]{1,0:T(8,128)(2,1)S(1)} %copy-done, bf16[2048,768]{1,0:T(8,128)(2,1)} %butterfly.1.leaves), custom_call_target="tpu_custom_call" | custom-call | tf_op jit(solution)/shard_map/decode/pallas_call | solution.py:318
Async XLA Ops:
  0.0 65.5 %copy-start = (bf16[2048,256]{1,0:T(8,128)(2,1)S(1)}, bf16[2048,256]{1,0:T(8,128)(2,1)}, u32[]{:S(2)}) copy-start(bf16[2048,256]{1,0:T(8,128)(2,1)} %dec.1) | copy-start | bytes 3145732
